TPU v7x, 32 devices: a whole 2x2x4 slice. The times are simulated.
32 devices in a mesh: grp: 4 (over y, x), seq: 8 (over z, core).
Axes of the slice: x: 2, y: 2, z: 4, core: 2. Of those that a mesh axis runs over, the one named last changes fastest.
Arguments:
- tokens: bfloat16 [2048, 8192], P(None, 'seq'), may hold values from -16 to 16
- proj_weight: bfloat16 [8192, 5120], P('seq', 'grp'), may hold values from -0.0625 to 0.0625
- proj_bias: bfloat16 [5120], P('grp'), may hold values from -3 to 3
- out_weight: bfloat16 [4096, 8192], P('grp'), may hold values from -0.125 to 0.125
- doc_ids: int32 [2048], P('seq'), may hold values from 0 to 2, never falling along the last dimension, each value on 1 to 1280 neighbouring positions
Outputs:
- mixed: bfloat16 [2048, 8192], P('seq', 'grp')
Inputs may be any that keep to these rules, and one draw needn't show every extreme that they name: `doc_ids`: numbers never fall along the sequence; every document has 1 to 1280 tokens, one exactly that many; every number up to 2 is used.
All inputs are finite; a program needn't handle non-finite values.
Results may differ from a plain program's by a relative error of at most 0.012.
Values may be sent and summed in bfloat16 or wider, within the bound.
A program may use at most 256 MiB of HBM per device.

v0:
```python
import jax
import jax.numpy as jnp
from jax import lax
from jax.sharding import PartitionSpec as P

HEAD_DIM = 128
GQA = 8
theta_base = 1000000.0
neg_large = -1e30


def rotate(inputs, positions, head_dim):
    half_dim = head_dim // 2
    inverse_freq = theta_base ** (-(jnp.arange(half_dim, dtype=jnp.float32) * 2.0) / head_dim)
    angles = positions.astype(jnp.float32)[:, None] * inverse_freq[None, :]
    cosine = jnp.concatenate([jnp.cos(angles), jnp.cos(angles)], axis=1)
    sine_table = jnp.concatenate([jnp.sin(angles), jnp.sin(angles)], axis=1)
    low_half = inputs[..., :half_dim]
    high_half = inputs[..., half_dim:]
    turned = jnp.concatenate([-high_half, low_half], axis=-1)
    return inputs * cosine[:, None, :] + turned * sine_table[:, None, :]


def body(tokens, proj_weight, proj_bias, out_weight, doc_ids):
    tok_rows = doc_ids.shape[0]
    kv_local = proj_weight.shape[1] // ((GQA + 2) * HEAD_DIM)
    my_start = lax.axis_index("seq") * tok_rows
    projected = lax.psum_scatter(
        jnp.dot(tokens, proj_weight, preferred_element_type=jnp.float32),
        "seq",
        scatter_dimension=0,
        tiled=True,
    )
    projected = projected + proj_bias.astype(jnp.float32)[None, :]
    projected = projected.reshape(tok_rows, kv_local, GQA + 2, HEAD_DIM)
    positions = my_start + jnp.arange(tok_rows, dtype=jnp.int32)
    queries = rotate(
        projected[:, :, :GQA, :].reshape(tok_rows, kv_local * GQA, HEAD_DIM), positions, HEAD_DIM
    )
    queries = queries.astype(jnp.bfloat16).reshape(tok_rows, kv_local, GQA, HEAD_DIM)
    key_rows = rotate(projected[:, :, GQA, :], positions, HEAD_DIM).astype(jnp.bfloat16)
    value_rows = projected[:, :, GQA + 1, :].astype(jnp.bfloat16)
    score_scale = HEAD_DIM ** (-0.5)
    initial = (
        jnp.full((kv_local, GQA, tok_rows), neg_large, jnp.float32),
        jnp.zeros((kv_local, GQA, tok_rows), jnp.float32),
        jnp.zeros((kv_local, GQA, tok_rows, HEAD_DIM), jnp.float32),
    )
    key_block = lax.all_gather(key_rows, "seq", axis=0, tiled=True)
    value_block = lax.all_gather(value_rows, "seq", axis=0, tiled=True)
    block_ids = lax.all_gather(doc_ids, "seq", axis=0, tiled=True)
    key_index = jnp.arange(block_ids.shape[0], dtype=jnp.int32)
    allowed = (
        (block_ids[None, :] == doc_ids[:, None])
        & (key_index[None, :] <= positions[:, None])
        & (key_index[None, :] >= 0)
    )

    def compute(state):
        row_max, row_sum, weighted = state
        scores = (
            jnp.einsum("qkgd,pkd->kgqp", queries, key_block, preferred_element_type=jnp.float32)
            * score_scale
        )
        scores = jnp.where(allowed[None, None], scores, neg_large)
        new_max = jnp.maximum(row_max, jnp.max(scores, axis=-1))
        weights = jnp.where(allowed[None, None], jnp.exp(scores - new_max[..., None]), 0.0)
        new_sum = jnp.sum(weights, axis=-1)
        update = jnp.einsum(
            "kgqp,pkd->kgqd",
            weights.astype(jnp.bfloat16),
            value_block,
            preferred_element_type=jnp.float32,
        )
        return (new_max, new_sum, update)

    folded = lax.cond(jnp.any(allowed), compute, lambda state: state, initial)
    row_max, row_sum, weighted = folded
    outputs = (weighted / row_sum[..., None]).astype(jnp.bfloat16)
    attended = jnp.transpose(outputs, (2, 0, 1, 3)).reshape(tok_rows, kv_local * GQA * HEAD_DIM)
    partial_value = jnp.dot(attended, out_weight, preferred_element_type=jnp.float32)
    return lax.psum_scatter(partial_value, "grp", scatter_dimension=1, tiled=True).astype(
        jnp.bfloat16
    )


def solution(mesh):
    return jax.shard_map(
        body,
        mesh=mesh,
        in_specs=(P(None, "seq"), P("seq", "grp"), P("grp"), P("grp", None), P("seq")),
        out_specs=P("seq", "grp"),
        check_vma=False,
    )
```

profile of v0, /device:TPU:0, one launch (start us, length us, event | category | flops | bytes accessed | tf_op | source)
XLA Modules:
  0.0 283.6 jit_solution(13679033153051287310)
XLA Ops:
  6.5 0.0 copy-start
  6.5 0.0 reduce-scatter.3.cloned.1.call-start
  6.5 1.7 copy-done
  8.3 9.7 %fusion.27 = f32[2048,1280]{1,0:T(8,128)} fusion(bf16[2048,1024]{1,0:T(8,128)(2,1)} %param.7, bf16[1024,1280]{1,0:T(8,128)(2,1)S(1)} %copy-done), kind=kOutput, calls=%fused_computation.45 | convolution fusion | flops 5368709120 | bytes 17301504 | tf_op jit(solution)/shard_map/dot_general | solution.py:29
  18.0 0.0 copy-start.3
  18.0 0.0 copy-start.2
  18.0 0.0 reduce-scatter.3.cloned.1.call-update
  18.0 0.0 reduce-scatter.5.cloned.1.call-start
  18.0 0.6 copy-done.3
  18.6 0.0 copy-done.2
  18.7 13.5 %all-gather.1 = s32[8,1,256]{2,1,0:T(1,128)S(1)} all-gather(s32[1,1,256]{2,1,0:T(1,128)S(1)} %bitcast.80), channel_id=1, replica_groups=mesh['grp'=4,'seq'=8] {'seq'}, dimensions={0}, use_global_device_ids=true | all-gather | bytes 9216 | tf_op jit(solution)/shard_map/all_gather | solution.py:51
  32.1 1.2 fusion.17
  34.0 0.3 multiply_cosine_fusion
  34.4 95.8 %reduce-scatter.3.cloned.1.call-done = f32[256,1280]{1,0:T(8,128)} async-done(((f32[2048,1280]{1,0:T(8,128)}), f32[256,1280]{1,0:T(8,128)}) %reduce-scatter.3.cloned.1.call-update) | async-done | bytes 1310736 | tf_op jit(solution)/shard_map/reduce_scatter | solution.py:28
  130.2 2.5 broadcast_add_fusion
  132.7 1.7 copy.17
  134.4 0.1 slice_bitcast_fusion
  134.6 14.8 %all_gather.10 = bf16[2048,1,128]{0,2,1:T(8,128)(2,1)S(1)} all-gather(bf16[256,1,128]{0,2,1:T(8,128)(2,1)S(1)} %fusion.22), channel_id=1, replica_groups=mesh['grp'=4,'seq'=8] {'seq'}, dimensions={0}, use_global_device_ids=true | all-gather | bytes 589824 | tf_op jit(solution)/shard_map/all_gather | solution.py:49
  149.4 14.9 %all-gather = bf16[2048,1,1,128]{0,3,2,1:T(8,128)(2,1)S(1)} all-gather(bf16[256,1,1,128]{0,3,2,1:T(8,128)(2,1)S(1)} %slice.47), channel_id=2, replica_groups=mesh['grp'=4,'seq'=8] {'seq'}, dimensions={0}, use_global_device_ids=true | all-gather | bytes 589824 | tf_op jit(solution)/shard_map/all_gather | solution.py:50
  164.3 0.1 fusion.20
  164.4 0.2 fusion.19
  164.6 11.5 %conditional.1 = (f32[1,8,256]{2,1,0:T(8,128)S(1)}, f32[1,8,256,128]{2,3,1,0:T(8,128)S(1)}) conditional(s32[]{:T(128)} %convert_element_type.50, () %tuple.13, (pred[256,2048]{0,1:T(8,128)(4,1)S(1)}, bf16[2048,1,128]{0,2,1:T(8,128)(2,1)S(1)}, bf16[256,1,8,128]{0,3,2,1:T(8,128)(2,1)S(1)}, bf16[2048,1,128]{0,2,1:T(8,128)(2,1)S(1)}) %tuple.33), branch_computations={%region_2.0_spmd, %region_3.6_spmd} | conditional | flops 2202007552 | bytes 54575120 | solution.py:77
  164.6 2.7 fusion
  167.4 4.0 %fusion.2 = f32[8,256]{1,0:T(8,128)S(1)} fusion(f32[2048,256,8]{1,0,2:T(8,128)S(1)} %get-tuple-element.31, f32[8,256]{1,0:T(8,128)S(1)} %broadcast_maximum_fusion, pred[256,2048]{0,1:T(8,128)(4,1)S(1)} %get-tuple-element.13), kind=kLoop, calls=%fused_computation.4 | loop fusion | flops 20969472 | bytes 17317888 | tf_op jit(solution)/shard_map/cond/branch_1_fun/reduce_sum | solution.py:68
  171.4 4.5 %fusion.7 = f32[1,8,256,128]{2,3,1,0:T(8,128)S(1)} fusion(f32[2048,256,8]{1,0,2:T(8,128)S(1)} %get-tuple-element.31, f32[8,256]{1,0:T(8,128)S(1)} %broadcast_maximum_fusion, pred[256,2048]{0,1:T(8,128)(4,1)S(1)} %get-tuple-element.13, bf16[2048,1,128]{0,2,1:T(8,128)(2,1)S(1)} %get-tuple-element.28), kind=kOutput, calls=%fused_computation.8 | convolution fusion | flops 1094713344 | bytes 18882560 | tf_op jit(solution)/shard_map/cond/branch_1_fun/kgqp,pkd->kgqd/dot_general | solution.py:69
  176.1 0.1 divide_convert_fusion
  176.2 0.0 copy-start.1
  176.2 12.9 %fusion.28 = f32[256,8192]{1,0:T(8,128)} fusion(bf16[256,1024]{0,1:T(8,128)(2,1)S(1)} %bitcast.75, bf16[1024,8192]{1,0:T(8,128)(2,1)} %param.10), kind=kOutput, calls=%fused_computation.46 | convolution fusion | flops 4294967296 | bytes 25690112 | tf_op jit(solution)/shard_map/dot_general | solution.py:81
  189.1 0.0 reduce-scatter.5.cloned.1.call-update
  189.1 85.0 %reduce-scatter.5.cloned.1.call-done = f32[256,2048]{1,0:T(8,128)} async-done(((f32[256,8192]{1,0:T(8,128)}), f32[256,2048]{1,0:T(8,128)}) %reduce-scatter.5.cloned.1.call-update) | async-done | bytes 2097168 | tf_op jit(solution)/shard_map/reduce_scatter | solution.py:82
  274.1 2.7 convert_element_type.57
  276.8 0.0 copy-done.1
  (10 shorter events, 0.1 us)
Async XLA Ops:
  6.5 1.7 copy-start
  6.5 123.7 %reduce-scatter.3.cloned.1.call-start = ((), (), s32[]{:S(2)}) async-start(), calls=%async_computation.2 | async-start | bytes 11796480 | tf_op jit(solution)/shard_map/reduce_scatter | solution.py:28
  18.0 0.7 copy-start.3
  18.0 0.7 copy-start.2
  18.0 256.1 %reduce-scatter.5.cloned.1.call-start = ((), (), s32[]{:S(2)}) async-start(), calls=%async_computation.3 | async-start | bytes 10485760 | tf_op jit(solution)/shard_map/reduce_scatter | solution.py:82
  176.2 100.6 %copy-start.1 = (bf16[1024,1280]{1,0:T(8,128)(2,1)S(1)}, bf16[1024,1280]{1,0:T(8,128)(2,1)}, u32[]{:S(2)}) copy-start(bf16[1024,1280]{1,0:T(8,128)(2,1)} %param.8) | copy-start | bytes 7864324
Sparse Core Ops, SparseCore 0:
  18.1 112.0 reduce-scatter.2
  189.2 84.8 reduce-scatter.4
where the time goes:
time: 284 us
  waiting for transfers between devices  181 us (64%)
  blocking collectives  43.2 us (15%)
  matrix products  29.8 us (10%)
  between operations  14.2 us (5%)
  other arithmetic  11.2 us (4%)
  local copies, waits for them, and re-layouts  4.16 us (1%)
    reduce_scatter x1, waiting for transfers between devices, body(): lax.psum_scatter(jnp.dot(tokens, proj_weight, preferred_element_type=jnp....  95.8 us
    reduce_scatter x1, waiting for transfers between devices, body(): lax.psum_scatter(partial_value, 'grp', scatter_dimension=1, tiled=True)  85 us
    all_gather x1, blocking collectives, body(): value_block = lax.all_gather(value_rows, 'seq', axis=0, tiled=True)  14.9 us
    all_gather x1, blocking collectives, body(): key_block = lax.all_gather(key_rows, 'seq', axis=0, tiled=True)  14.8 us
    all_gather x1, blocking collectives, body(): block_ids = lax.all_gather(doc_ids, 'seq', axis=0, tiled=True)  13.5 us
    dot_general x1, matrix products, body(): jnp.dot(attended, out_weight, preferred_element_type=jnp.float32)  12.9 us
    dot_general x1, matrix products, body(): jnp.dot(tokens, proj_weight, preferred_element_type=jnp.float32)  9.68 us
  transfers between devices with their start and end apart: 2, of which 2 were waited for; matrix products, arithmetic and copies ran while one was open for 1% of the time, Pallas kernels for 0%

commit v1 on v0

--- a/solution.py
+++ b/solution.py
@@ -46,7 +46,12 @@
         jnp.zeros((kv_local, GQA, tok_rows), jnp.float32),
         jnp.zeros((kv_local, GQA, tok_rows, HEAD_DIM), jnp.float32),
     )
-    key_block = lax.all_gather(key_rows, "seq", axis=0, tiled=True)
+    ring = [key_rows]
+    for hop in range(7):
+        ring.append(lax.ppermute(ring[-1], "seq", [(dev, (dev + 1) % 8) for dev in range(8)]))
+    key_block = jnp.roll(
+        jnp.concatenate(ring[::-1], axis=0), (lax.axis_index("seq") + 1) * ring[0].shape[0], axis=0
+    )
     value_block = lax.all_gather(value_rows, "seq", axis=0, tiled=True)
     block_ids = lax.all_gather(doc_ids, "seq", axis=0, tiled=True)
     key_index = jnp.arange(block_ids.shape[0], dtype=jnp.int32)

time: 284 us -> 311 us (1.095)
  waiting for transfers between devices: 181 us -> 213 us
  blocking collectives: 43.2 us -> 28.3 us
  local copies, waits for them, and re-layouts: 4.16 us -> 14.6 us
    ppermute x0 -> x7, waiting for transfers between devices: none -> 30.6 us  [body(): lax.ppermute(ring[-1], 'seq', [(dev, (dev + 1) % 8) for dev in range(8)])]
    all_gather x1 -> x0, blocking collectives: 14.8 us -> none  [body(): key_block = lax.all_gather(key_rows, 'seq', axis=0, tiled=True)]
    unnamed x8 -> x23, local copies, waits for them, and re-layouts: 2.36 us -> 11.9 us
  transfers between devices with their start and end apart: 2 -> 9, of which waited for: 2 -> 8; matrix products, arithmetic and copies ran while one was open for 1% -> 1% of each run, Pallas kernels for 0% -> 0%
where the time goes in v1:
time: 311 us
  waiting for transfers between devices  213 us (68%)
  matrix products  29.7 us (10%)
  blocking collectives  28.3 us (9%)
  local copies, waits for them, and re-layouts  14.6 us (5%)
  between operations  14.2 us (5%)
  other arithmetic  10.2 us (3%)
    reduce_scatter x1, waiting for transfers between devices, body(): lax.psum_scatter(jnp.dot(tokens, proj_weight, preferred_element_type=jnp....  97.7 us
    reduce_scatter x1, waiting for transfers between devices, body(): lax.psum_scatter(partial_value, 'grp', scatter_dimension=1, tiled=True)  84.8 us
    ppermute x7, waiting for transfers between devices, body(): lax.ppermute(ring[-1], 'seq', [(dev, (dev + 1) % 8) for dev in range(8)])  30.6 us
    all_gather x1, blocking collectives, body(): value_block = lax.all_gather(value_rows, 'seq', axis=0, tiled=True)  14.8 us
    all_gather x1, blocking collectives, body(): block_ids = lax.all_gather(doc_ids, 'seq', axis=0, tiled=True)  13.5 us
    dot_general x1, matrix products, body(): jnp.dot(attended, out_weight, preferred_element_type=jnp.float32)  12.9 us
    unnamed x23, local copies, waits for them, and re-layouts  11.9 us
    dot_general x1, matrix products, body(): jnp.dot(tokens, proj_weight, preferred_element_type=jnp.float32)  9.68 us
  transfers between devices with their start and end apart: 9, of which 8 were waited for; matrix products, arithmetic and copies ran while one was open for 1% of the time, Pallas kernels for 0%

profile of v1, /device:TPU:0, one launch (start us, length us, event | category | flops | bytes accessed | tf_op | source)
XLA Modules:
  0.0 310.5 jit_solution(2219195163523747733)
XLA Ops:
  6.5 0.0 copy-start
  6.5 0.0 reduce-scatter.3.cloned.1.call-start
  6.5 1.7 copy-done
  8.3 9.7 %fusion.29 = f32[2048,1280]{1,0:T(8,128)} fusion(bf16[2048,1024]{1,0:T(8,128)(2,1)} %param.7, bf16[1024,1280]{1,0:T(8,128)(2,1)S(1)} %copy-done), kind=kOutput, calls=%fused_computation.63 | convolution fusion | flops 5368709120 | bytes 17301504 | tf_op jit(solution)/shard_map/dot_general | solution.py:29
  18.0 0.0 copy-start.3
  18.0 0.0 copy-start.2
  18.0 0.0 reduce-scatter.3.cloned.1.call-update
  18.0 0.0 reduce-scatter.5.cloned.1.call-start
  18.0 0.6 copy-done.3
  18.6 0.0 copy-done.2
  18.7 13.5 %all-gather.1 = s32[8,1,256]{2,1,0:T(1,128)S(1)} all-gather(s32[1,1,256]{2,1,0:T(1,128)S(1)} %bitcast.86), channel_id=1, replica_groups=mesh['grp'=4,'seq'=8] {'seq'}, dimensions={0}, use_global_device_ids=true | all-gather | bytes 9216 | tf_op jit(solution)/shard_map/all_gather | solution.py:56
  32.1 0.3 multiply_cosine_fusion
  32.5 97.7 %reduce-scatter.3.cloned.1.call-done = f32[256,1280]{1,0:T(8,128)} async-done(((f32[2048,1280]{1,0:T(8,128)}), f32[256,1280]{1,0:T(8,128)}) %reduce-scatter.3.cloned.1.call-update) | async-done | bytes 1310736 | tf_op jit(solution)/shard_map/reduce_scatter | solution.py:28
  130.2 1.4 broadcast_add_fusion
  131.6 0.4 copy.17
  132.1 0.1 collective-permute-start
  132.2 5.5 %collective-permute-done = bf16[256,1,128]{0,2,1:T(8,128)(2,1)S(1)} collective-permute-done((bf16[256,1,128]{0,2,1:T(8,128)(2,1)S(1)}, bf16[256,1,128]{0,2,1:T(8,128)(2,1)S(1)}, u32[]{:S(2)}, u32[]{:S(2)}) %collective-permute-start) | collective-permute-done | bytes 65568 | tf_op jit(solution)/shard_map/ppermute | solution.py:51
  137.6 0.0 collective-permute-start.1
  137.6 1.2 fusion.19
  139.5 3.6 %collective-permute-done.1 = bf16[256,1,128]{0,2,1:T(8,128)(2,1)S(1)} collective-permute-done((bf16[256,1,128]{0,2,1:T(8,128)(2,1)S(1)}, bf16[256,1,128]{0,2,1:T(8,128)(2,1)S(1)}, u32[]{:S(2)}, u32[]{:S(2)}) %collective-permute-start.1) | collective-permute-done | bytes 65568 | tf_op jit(solution)/shard_map/ppermute | solution.py:51
  143.1 0.0 collective-permute-start.2
  143.1 5.5 %collective-permute-done.2 = bf16[256,1,128]{0,2,1:T(8,128)(2,1)S(1)} collective-permute-done((bf16[256,1,128]{0,2,1:T(8,128)(2,1)S(1)}, bf16[256,1,128]{0,2,1:T(8,128)(2,1)S(1)}, u32[]{:S(2)}, u32[]{:S(2)}) %collective-permute-start.2) | collective-permute-done | bytes 65568 | tf_op jit(solution)/shard_map/ppermute | solution.py:51
  148.6 0.0 collective-permute-start.3
  148.6 0.1 slice_bitcast_fusion
  148.7 5.4 %collective-permute-done.3 = bf16[256,1,128]{0,2,1:T(8,128)(2,1)S(1)} collective-permute-done((bf16[256,1,128]{0,2,1:T(8,128)(2,1)S(1)}, bf16[256,1,128]{0,2,1:T(8,128)(2,1)S(1)}, u32[]{:S(2)}, u32[]{:S(2)}) %collective-permute-start.3) | collective-permute-done | bytes 65568 | tf_op jit(solution)/shard_map/ppermute | solution.py:51
  154.1 0.0 collective-permute-start.4
  154.1 0.1 fusion.22
  154.2 5.4 %collective-permute-done.4 = bf16[256,1,128]{0,2,1:T(8,128)(2,1)S(1)} collective-permute-done((bf16[256,1,128]{0,2,1:T(8,128)(2,1)S(1)}, bf16[256,1,128]{0,2,1:T(8,128)(2,1)S(1)}, u32[]{:S(2)}, u32[]{:S(2)}) %collective-permute-start.4) | collective-permute-done | bytes 65568 | tf_op jit(solution)/shard_map/ppermute | solution.py:51
  159.6 0.0 collective-permute-start.5
  159.6 0.2 fusion.21
  159.8 5.3 %collective-permute-done.5 = bf16[256,1,128]{0,2,1:T(8,128)(2,1)S(1)} collective-permute-done((bf16[256,1,128]{0,2,1:T(8,128)(2,1)S(1)}, bf16[256,1,128]{0,2,1:T(8,128)(2,1)S(1)}, u32[]{:S(2)}, u32[]{:S(2)}) %collective-permute-start.5) | collective-permute-done | bytes 65568 | tf_op jit(solution)/shard_map/ppermute | solution.py:51
  165.1 0.0 collective-permute-start.6
  165.1 14.8 %all-gather = bf16[2048,1,1,128]{0,3,2,1:T(8,128)(2,1)S(1)} all-gather(bf16[256,1,1,128]{0,3,2,1:T(8,128)(2,1)S(1)} %slice.47), channel_id=2, replica_groups=mesh['grp'=4,'seq'=8] {'seq'}, dimensions={0}, use_global_device_ids=true | all-gather | bytes 589824 | tf_op jit(solution)/shard_map/all_gather | solution.py:55
  180.0 0.0 collective-permute-done.6
  180.0 0.6 constant_dynamic-update-slice_fusion.15
  180.6 0.6 constant_dynamic-update-slice_fusion.14
  181.2 0.6 constant_dynamic-update-slice_fusion.13
  181.9 0.6 constant_dynamic-update-slice_fusion.12
  182.5 0.6 constant_dynamic-update-slice_fusion.11
  183.1 0.6 constant_dynamic-update-slice_fusion.10
  183.8 0.6 constant_dynamic-update-slice_fusion.9
  184.4 0.6 constant_dynamic-update-slice_fusion.8
  185.0 0.6 constant_dynamic-update-slice_fusion.7
  185.7 0.6 constant_dynamic-update-slice_fusion.6
  186.3 0.6 constant_dynamic-update-slice_fusion.5
  187.0 0.6 constant_dynamic-update-slice_fusion.4
  187.6 0.6 constant_dynamic-update-slice_fusion.3
  188.2 0.6 constant_dynamic-update-slice_fusion.2
  188.9 0.6 constant_dynamic-update-slice_fusion.1
  189.5 0.6 constant_dynamic-update-slice_fusion
  190.1 13.0 %conditional.1 = (f32[1,8,256]{2,1,0:T(8,128)S(1)}, f32[1,8,256,128]{2,3,1,0:T(8,128)S(1)}) conditional(s32[]{:T(128)} %convert_element_type.53, () %tuple.24, (pred[256,2048]{0,1:T(8,128)(4,1)S(1)}, s32[]{:T(128)}, bf16[4096,1,128]{0,2,1:T(8,128)(2,1)}, bf16[256,1,8,128]{0,3,2,1:T(8,128)(2,1)S(1)}, bf16[2048,1,128]{0,2,1:T(8,128)(2,1)S(1)}, ...), branch_computations={%region_2.3_spmd, %region_3.6_spmd.clone.clone} | conditional | flops 2202007552 | bytes 56672432 | solution.py:82
  190.1 1.6 copy.25
  191.7 2.7 fusion
  194.4 4.0 %fusion.2 = f32[8,256]{1,0:T(8,128)S(1)} fusion(f32[2048,256,8]{1,0,2:T(8,128)S(1)} %get-tuple-element.164, f32[8,256]{1,0:T(8,128)S(1)} %broadcast_maximum_fusion, pred[256,2048]{0,1:T(8,128)(4,1)S(1)} %get-tuple-element.149), kind=kLoop, calls=%fused_computation.4 | loop fusion | flops 20969472 | bytes 17317888 | tf_op jit(solution)/shard_map/cond/branch_1_fun/reduce_sum | solution.py:73
  198.5 4.5 %fusion.7 = f32[1,8,256,128]{2,3,1,0:T(8,128)S(1)} fusion(f32[2048,256,8]{1,0,2:T(8,128)S(1)} %get-tuple-element.164, f32[8,256]{1,0:T(8,128)S(1)} %broadcast_maximum_fusion, pred[256,2048]{0,1:T(8,128)(4,1)S(1)} %get-tuple-element.149, bf16[2048,1,128]{0,2,1:T(8,128)(2,1)S(1)} %get-tuple-element.152), kind=kOutput, calls=%fused_computation.8 | convolution fusion | flops 1094713344 | bytes 18882560 | tf_op jit(solution)/shard_map/cond/branch_1_fun/kgqp,pkd->kgqd/dot_general | solution.py:74
  203.1 0.1 divide_convert_fusion
  203.2 0.0 copy-start.1
  203.2 12.9 %fusion.30 = f32[256,8192]{1,0:T(8,128)} fusion(bf16[256,1024]{0,1:T(8,128)(2,1)S(1)} %bitcast.81, bf16[1024,8192]{1,0:T(8,128)(2,1)} %param.10), kind=kOutput, calls=%fused_computation.64 | convolution fusion | flops 4294967296 | bytes 25690112 | tf_op jit(solution)/shard_map/dot_general | solution.py:86
  216.1 0.0 reduce-scatter.5.cloned.1.call-update
  216.2 84.8 %reduce-scatter.5.cloned.1.call-done = f32[256,2048]{1,0:T(8,128)} async-done(((f32[256,8192]{1,0:T(8,128)}), f32[256,2048]{1,0:T(8,128)}) %reduce-scatter.5.cloned.1.call-update) | async-done | bytes 2097168 | tf_op jit(solution)/shard_map/reduce_scatter | solution.py:87
  301.0 2.7 convert_element_type.60
  303.7 0.0 copy-done.1
  (10 shorter events, 0.1 us)
Async XLA Ops:
  6.5 1.7 copy-start
  6.5 123.7 %reduce-scatter.3.cloned.1.call-start = ((), (), s32[]{:S(2)}) async-start(), calls=%async_computation.2 | async-start | bytes 11796480 | tf_op jit(solution)/shard_map/reduce_scatter | solution.py:28
  18.0 0.7 copy-start.3
  18.0 0.7 copy-start.2
  18.0 283.0 %reduce-scatter.5.cloned.1.call-start = ((), (), s32[]{:S(2)}) async-start(), calls=%async_computation.3 | async-start | bytes 10485760 | tf_op jit(solution)/shard_map/reduce_scatter | solution.py:87
  132.1 5.5 %collective-permute-start = (bf16[256,1,128]{0,2,1:T(8,128)(2,1)S(1)}, bf16[256,1,128]{0,2,1:T(8,128)(2,1)S(1)}, u32[]{:S(2)}, u32[]{:S(2)}) collective-permute-start(bf16[256,1,128]{0,2,1:T(8,128)(2,1)S(1)} %fusion.24), channel_id=1, source_target_pairs={{0,1},{1,2},{2,3},{3,4},{4,5},{5,6},{6,7},{7,0},{8,9},{9,10},{10,1... | collective-permute-start | bytes 196616 | tf_op jit(solution)/shard_map/ppermute | solution.py:51
  137.6 5.5 %collective-permute-start.1 = (bf16[256,1,128]{0,2,1:T(8,128)(2,1)S(1)}, bf16[256,1,128]{0,2,1:T(8,128)(2,1)S(1)}, u32[]{:S(2)}, u32[]{:S(2)}) collective-permute-start(bf16[256,1,128]{0,2,1:T(8,128)(2,1)S(1)} %collective-permute-done), channel_id=1, source_target_pairs={{0,1},{1,2},{2,3},{3,4},{4,5},{5,6},{6,7},{7,0},{8,9},{9,10},{10,1... | collective-permute-start | bytes 196616 | tf_op jit(solution)/shard_map/ppermute | solution.py:51
  143.1 5.5 %collective-permute-start.2 = (bf16[256,1,128]{0,2,1:T(8,128)(2,1)S(1)}, bf16[256,1,128]{0,2,1:T(8,128)(2,1)S(1)}, u32[]{:S(2)}, u32[]{:S(2)}) collective-permute-start(bf16[256,1,128]{0,2,1:T(8,128)(2,1)S(1)} %collective-permute-done.1), channel_id=1, source_target_pairs={{0,1},{1,2},{2,3},{3,4},{4,5},{5,6},{6,7},{7,0},{8,9},{9,10},{10,1... | collective-permute-start | bytes 196616 | tf_op jit(solution)/shard_map/ppermute | solution.py:51
  148.6 5.5 %collective-permute-start.3 = (bf16[256,1,128]{0,2,1:T(8,128)(2,1)S(1)}, bf16[256,1,128]{0,2,1:T(8,128)(2,1)S(1)}, u32[]{:S(2)}, u32[]{:S(2)}) collective-permute-start(bf16[256,1,128]{0,2,1:T(8,128)(2,1)S(1)} %collective-permute-done.2), channel_id=1, source_target_pairs={{0,1},{1,2},{2,3},{3,4},{4,5},{5,6},{6,7},{7,0},{8,9},{9,10},{10,1... | collective-permute-start | bytes 196616 | tf_op jit(solution)/shard_map/ppermute | solution.py:51
  154.1 5.5 %collective-permute-start.4 = (bf16[256,1,128]{0,2,1:T(8,128)(2,1)S(1)}, bf16[256,1,128]{0,2,1:T(8,128)(2,1)S(1)}, u32[]{:S(2)}, u32[]{:S(2)}) collective-permute-start(bf16[256,1,128]{0,2,1:T(8,128)(2,1)S(1)} %collective-permute-done.3), channel_id=1, source_target_pairs={{0,1},{1,2},{2,3},{3,4},{4,5},{5,6},{6,7},{7,0},{8,9},{9,10},{10,1... | collective-permute-start | bytes 196616 | tf_op jit(solution)/shard_map/ppermute | solution.py:51
  159.6 5.5 %collective-permute-start.5 = (bf16[256,1,128]{0,2,1:T(8,128)(2,1)S(1)}, bf16[256,1,128]{0,2,1:T(8,128)(2,1)S(1)}, u32[]{:S(2)}, u32[]{:S(2)}) collective-permute-start(bf16[256,1,128]{0,2,1:T(8,128)(2,1)S(1)} %collective-permute-done.4), channel_id=1, source_target_pairs={{0,1},{1,2},{2,3},{3,4},{4,5},{5,6},{6,7},{7,0},{8,9},{9,10},{10,1... | collective-permute-start | bytes 196616 | tf_op jit(solution)/shard_map/ppermute | solution.py:51
  165.1 14.8 %collective-permute-start.6 = (bf16[256,1,128]{0,2,1:T(8,128)(2,1)S(1)}, bf16[256,1,128]{0,2,1:T(8,128)(2,1)S(1)}, u32[]{:S(2)}, u32[]{:S(2)}) collective-permute-start(bf16[256,1,128]{0,2,1:T(8,128)(2,1)S(1)} %collective-permute-done.5), channel_id=1, source_target_pairs={{0,1},{1,2},{2,3},{3,4},{4,5},{5,6},{6,7},{7,0},{8,9},{9,10},{10,1... | collective-permute-start | bytes 196616 | tf_op jit(solution)/shard_map/ppermute | solution.py:51
  203.2 100.5 %copy-start.1 = (bf16[1024,1280]{1,0:T(8,128)(2,1)S(1)}, bf16[1024,1280]{1,0:T(8,128)(2,1)}, u32[]{:S(2)}) copy-start(bf16[1024,1280]{1,0:T(8,128)(2,1)} %param.8) | copy-start | bytes 7864324
Sparse Core Ops, SparseCore 0:
  18.1 112.0 reduce-scatter.2
  216.3 84.6 reduce-scatter.4
